TPU v7x, 32 devices: a whole 2x2x4 slice. The times are simulated.
32 devices in a mesh: dp: 8 (over z, y), tensor: 4 (over x, core).
Axes of the slice: x: 2, y: 2, z: 4, core: 2. Of those that a mesh axis runs over, the one named last changes fastest.
Arguments:
- tokens: bfloat16 [12288, 1024], P('dp', 'tensor'), may hold values from -6 to 6
- segment_ids: int32 [12288], P('dp'), may hold values from 0 to 8, as said below
- w_query: bfloat16 [1024, 1024], P(None, 'tensor'), may hold values from -0.1875 to 0.1875
- w_key: bfloat16 [1024, 1024], P(None, 'tensor'), may hold values from -0.1875 to 0.1875
- w_value: bfloat16 [1024, 1024], P(None, 'tensor'), may hold values from -0.1875 to 0.1875
- b_query: bfloat16 [1024], P('tensor'), may hold values from -3 to 3
- b_value: bfloat16 [1024], P('tensor'), may hold values from -3 to 3
- w_out: bfloat16 [1024, 1024], P('tensor'), may hold values from -0.75 to 0.75
- b_out: bfloat16 [1024], P('tensor'), may hold values from -3 to 3
- gain_one: bfloat16 [1024], P('tensor'), may hold values from 0.5 to 1.5
- bias_one: bfloat16 [1024], P('tensor'), may hold values from -3 to 3
- w_in: bfloat16 [1024, 4096], P(None, 'tensor'), may hold values from -0.1875 to 0.1875
- b_in: bfloat16 [4096], P('tensor'), may hold values from -3 to 3
- w_down: bfloat16 [4096, 1024], P('tensor'), may hold values from -0.09375 to 0.09375
- b_down: bfloat16 [1024], P('tensor'), may hold values from -3 to 3
- gain_two: bfloat16 [1024], P('tensor'), may hold values from 0.5 to 1.5
- bias_two: bfloat16 [1024], P('tensor'), may hold values from -3 to 3
- cotangent: bfloat16 [12288, 1024], P('dp', 'tensor'), may hold values from -6 to 6
Outputs:
- out: bfloat16 [12288, 1024], P('dp', 'tensor')
- grad_tokens: bfloat16 [12288, 1024], P('dp', 'tensor')
- grad_w_query: float32 [1024, 1024], P(None, 'tensor')
- grad_w_key: float32 [1024, 1024], P(None, 'tensor')
- grad_w_value: float32 [1024, 1024], P(None, 'tensor')
- grad_b_query: float32 [1024], P('tensor')
- grad_b_value: float32 [1024], P('tensor')
- grad_w_out: float32 [1024, 1024], P('tensor')
- grad_b_out: float32 [1024], P('tensor')
- grad_gain_one: float32 [1024], P('tensor')
- grad_bias_one: float32 [1024], P('tensor')
- grad_w_in: float32 [1024, 4096], P(None, 'tensor')
- grad_b_in: float32 [4096], P('tensor')
- grad_w_down: float32 [4096, 1024], P('tensor')
- grad_b_down: float32 [1024], P('tensor')
- grad_gain_two: float32 [1024], P('tensor')
- grad_bias_two: float32 [1024], P('tensor')
Inputs may be any that keep to these rules, and one draw needn't show every extreme that they name: `segment_ids`: within each packed sequence of 512 tokens the ids run from 1 to 8 without falling, each id on at least one token, followed by one or more tail slots of id 0.
All inputs are finite; a program needn't handle non-finite values.
Results may differ from a plain program's by a relative error of at most 0.015.
Values may be sent and summed in bfloat16 or wider, within the bound.
No kernel may reach another device: no remote copies, remote signals or barrier semaphores. Data moves between devices by JAX's collectives and lax.ppermute only.
A program may use at most 128 MiB of HBM per device.

v0:
```python
import jax
import jax.numpy as jnp
from jax import lax
from jax.sharding import PartitionSpec as P

HD = 64
LEN = 512
epsilon = 1e-05
masked_fill = -1000000000.0


def over_rows(left, right):
    return lax.dot_general(
        left, right, (((0,), (0,)), ((), ())), preferred_element_type=jnp.float32
    )


def against(left, right):
    return lax.dot_general(
        left, right, (((1,), (1,)), ((), ())), preferred_element_type=jnp.float32
    )


def allowed_pairs(labels):
    length = labels.shape[0]
    same_label = labels[:, None] == labels[None, :]
    diagonal = lax.broadcasted_iota(jnp.int32, (length, length), 0) == lax.broadcasted_iota(
        jnp.int32, (length, length), 1
    )
    return same_label & ((labels[:, None] != 0) | diagonal)


def masked_scores(query_rows, key_rows, labels):
    score_scale = query_rows.shape[-1] ** (-0.5)
    scores = (
        jnp.einsum("qhd,khd->hqk", query_rows, key_rows, preferred_element_type=jnp.float32)
        * score_scale
    )
    return (jnp.where(allowed_pairs(labels)[None], scores, masked_fill), score_scale)


def attend_block(sliced):
    query_rows, key_rows, value_rows, labels = sliced
    scores, score_scale = masked_scores(query_rows, key_rows, labels)
    row_peak = jnp.max(scores, axis=-1, keepdims=True)
    exp_terms = jnp.exp(scores - row_peak)
    exp_total = jnp.sum(exp_terms, axis=-1, keepdims=True)
    probs = (exp_terms / exp_total).astype(jnp.bfloat16)
    context = jnp.einsum("hqk,khd->qhd", probs, value_rows, preferred_element_type=jnp.float32)
    return (context.astype(jnp.bfloat16), (row_peak + jnp.log(exp_total))[..., 0])


def attend_back(sliced):
    query_rows, key_rows, value_rows, labels, dcontext, log_total = sliced
    scores, score_scale = masked_scores(query_rows, key_rows, labels)
    probs = jnp.exp(scores - log_total[..., None])
    dprobs = jnp.einsum("qhd,khd->hqk", dcontext, value_rows, preferred_element_type=jnp.float32)
    row_delta = jnp.sum(probs * dprobs, axis=-1, keepdims=True)
    dscores = (probs * (dprobs - row_delta)).astype(jnp.bfloat16)
    dquery = (
        jnp.einsum("hqk,khd->qhd", dscores, key_rows, preferred_element_type=jnp.float32)
        * score_scale
    )
    dkey = (
        jnp.einsum("hqk,qhd->khd", dscores, query_rows, preferred_element_type=jnp.float32)
        * score_scale
    )
    dvalue = jnp.einsum(
        "hqk,qhd->khd", probs.astype(jnp.bfloat16), dcontext, preferred_element_type=jnp.float32
    )
    return (dquery.astype(jnp.bfloat16), dkey.astype(jnp.bfloat16), dvalue.astype(jnp.bfloat16))


def norm_from(values, row_sums, model_width):
    row_mean = row_sums[0] / model_width
    variance = row_sums[1] / model_width - row_mean * row_mean
    inv_std = lax.rsqrt(variance + epsilon)
    return ((values - row_mean[:, None]) * inv_std[:, None], inv_std)


def norm_back(scaled, normed, inv_std, row_sums, model_width):
    return inv_std[:, None] * (
        scaled - row_sums[0][:, None] / model_width - normed * row_sums[1][:, None] / model_width
    )


def summed(parts):
    return lax.psum(parts, "dp")


def local(
    tokens,
    segment_ids,
    w_query,
    w_key,
    w_value,
    b_query,
    b_value,
    w_out,
    b_out,
    gain_one,
    bias_one,
    w_in,
    b_in,
    w_down,
    b_down,
    gain_two,
    bias_two,
    cotangent,
):
    row_count = tokens.shape[0]
    model_width = w_query.shape[0]
    local_cols = w_query.shape[1]
    head_count = local_cols // HD
    seq_count = row_count // LEN
    proj_weight = jnp.concatenate([w_query, w_key, w_value], axis=1)
    proj_bias = jnp.concatenate(
        [
            b_query.astype(jnp.float32),
            jnp.zeros((local_cols,), jnp.float32),
            b_value.astype(jnp.float32),
        ]
    )
    inputs = lax.all_gather(tokens, "tensor", axis=1, tiled=True)
    projected = (
        jnp.dot(inputs, proj_weight, preferred_element_type=jnp.float32) + proj_bias
    ).astype(jnp.bfloat16)

    def heads_of(block):
        return block.reshape(seq_count, LEN, head_count, HD)

    queries = heads_of(projected[:, :local_cols])
    key_proj = heads_of(projected[:, local_cols : 2 * local_cols])
    value_proj = heads_of(projected[:, 2 * local_cols :])
    labels = segment_ids.reshape(seq_count, LEN)
    context, log_total = lax.map(attend_block, (queries, key_proj, value_proj, labels))
    context = context.reshape(row_count, local_cols)
    attn_mine = lax.psum_scatter(
        jnp.dot(context, w_out, preferred_element_type=jnp.float32),
        "tensor",
        scatter_dimension=1,
        tiled=True,
    )
    z_one = tokens.astype(jnp.float32) + attn_mine + b_out.astype(jnp.float32)
    sums_one = lax.psum((jnp.sum(z_one, axis=1), jnp.sum(z_one * z_one, axis=1)), "tensor")
    n_one, inv_one = norm_from(z_one, sums_one, model_width)
    h_one = n_one * gain_one.astype(jnp.float32) + bias_one.astype(jnp.float32)
    h_low = lax.all_gather(h_one.astype(jnp.bfloat16), "tensor", axis=1, tiled=True)
    pre_act = jnp.dot(h_low, w_in, preferred_element_type=jnp.float32) + b_in.astype(jnp.float32)
    hidden = jax.nn.gelu(pre_act, approximate=False).astype(jnp.bfloat16)
    feed_mine = lax.psum_scatter(
        jnp.dot(hidden, w_down, preferred_element_type=jnp.float32),
        "tensor",
        scatter_dimension=1,
        tiled=True,
    )
    z_two = h_one + feed_mine + b_down.astype(jnp.float32)
    sums_two = lax.psum((jnp.sum(z_two, axis=1), jnp.sum(z_two * z_two, axis=1)), "tensor")
    n_two, inv_two = norm_from(z_two, sums_two, model_width)
    result = (n_two * gain_two.astype(jnp.float32) + bias_two.astype(jnp.float32)).astype(
        jnp.bfloat16
    )
    grad_out = cotangent.astype(jnp.float32)
    grad_gain_two = jnp.sum(grad_out * n_two, axis=0)
    grad_bias_two = jnp.sum(grad_out, axis=0)
    scaled_two = grad_out * gain_two.astype(jnp.float32)
    back_two = lax.psum(
        (jnp.sum(scaled_two, axis=1), jnp.sum(scaled_two * n_two, axis=1)), "tensor"
    )
    dz_two = norm_back(scaled_two, n_two, inv_two, back_two, model_width)
    grad_b_down = jnp.sum(dz_two, axis=0)
    dz_two_low = lax.all_gather(dz_two.astype(jnp.bfloat16), "tensor", axis=1, tiled=True)
    grad_w_down = over_rows(hidden, dz_two_low)
    dhidden = against(dz_two_low, w_down)
    _, gelu_pull = jax.vjp(lambda value_in: jax.nn.gelu(value_in, approximate=False), pre_act)
    dpre = gelu_pull(dhidden)[0].astype(jnp.bfloat16)
    grad_w_in = over_rows(h_low, dpre)
    grad_b_in = jnp.sum(dpre.astype(jnp.float32), axis=0)
    dh_one = dz_two + lax.psum_scatter(
        against(dpre, w_in), "tensor", scatter_dimension=1, tiled=True
    )
    feed_grads = (grad_w_in, grad_b_in, grad_w_down, grad_b_down, grad_gain_two, grad_bias_two)
    grad_gain_one = jnp.sum(dh_one * n_one, axis=0)
    grad_bias_one = jnp.sum(dh_one, axis=0)
    scaled_one = dh_one * gain_one.astype(jnp.float32)
    back_one = lax.psum(
        (jnp.sum(scaled_one, axis=1), jnp.sum(scaled_one * n_one, axis=1)), "tensor"
    )
    dz_one = norm_back(scaled_one, n_one, inv_one, back_one, model_width)
    grad_b_out = jnp.sum(dz_one, axis=0)
    dz_one_low = lax.all_gather(dz_one.astype(jnp.bfloat16), "tensor", axis=1, tiled=True)
    grad_w_out = over_rows(context, dz_one_low)
    dcontext = heads_of(against(dz_one_low, w_out).astype(jnp.bfloat16))
    dquery, dkey, dvalue = lax.map(
        attend_back, (queries, key_proj, value_proj, labels, dcontext, log_total)
    )
    dprojected = jnp.concatenate(
        [
            dquery.reshape(row_count, local_cols),
            dkey.reshape(row_count, local_cols),
            dvalue.reshape(row_count, local_cols),
        ],
        axis=1,
    )
    grad_proj = over_rows(inputs, dprojected)
    grad_b_query = jnp.sum(dprojected[:, :local_cols].astype(jnp.float32), axis=0)
    grad_b_value = jnp.sum(dprojected[:, 2 * local_cols :].astype(jnp.float32), axis=0)
    input_part = lax.psum_scatter(
        against(dprojected, proj_weight).astype(jnp.bfloat16),
        "tensor",
        scatter_dimension=1,
        tiled=True,
    ).astype(jnp.float32)
    grad_tokens = (dz_one + input_part).astype(jnp.bfloat16)
    attention_grads = (
        grad_proj[:, :local_cols],
        grad_proj[:, local_cols : 2 * local_cols],
        grad_proj[:, 2 * local_cols :],
        grad_b_query,
        grad_b_value,
        grad_w_out,
        grad_b_out,
        grad_gain_one,
        grad_bias_one,
    )
    totals = tuple(summed(attention_grads + feed_grads))
    return (result, grad_tokens) + totals


def solution(mesh):
    placed = (
        P("dp", "tensor"),
        P("dp"),
        P(None, "tensor"),
        P(None, "tensor"),
        P(None, "tensor"),
        P("tensor"),
        P("tensor"),
        P("tensor", None),
        P("tensor"),
        P("tensor"),
        P("tensor"),
        P(None, "tensor"),
        P("tensor"),
        P("tensor", None),
        P("tensor"),
        P("tensor"),
        P("tensor"),
        P("dp", "tensor"),
    )
    return jax.shard_map(
        local,
        mesh=mesh,
        in_specs=placed,
        out_specs=(
            P("dp", "tensor"),
            P("dp", "tensor"),
            P(None, "tensor"),
            P(None, "tensor"),
            P(None, "tensor"),
            P("tensor"),
            P("tensor"),
            P("tensor", None),
            P("tensor"),
            P("tensor"),
            P("tensor"),
            P(None, "tensor"),
            P("tensor"),
            P("tensor", None),
            P("tensor"),
            P("tensor"),
            P("tensor"),
        ),
        check_vma=False,
    )
```

profile of v0, /device:TPU:0, one launch (start us, length us, event | category | flops | bytes accessed | tf_op | source)
XLA Modules:
  0.0 971.1 jit_solution(15447300485332187335)
XLA Ops:
  14.6 26.6 %all-gather.5.cloned.1.call-done = bf16[1536,1024]{1,0:T(8,128)(2,1)} async-done(((bf16[1536,256]{1,0:T(8,128)(2,1)}), bf16[1536,1024]{1,0:T(8,128)(2,1)}) %all-gather.5.cloned.1.call-update) | async-done | bytes 3145744 | tf_op jit(solution)/shard_map/all_gather | solution.py:124
  41.2 5.2 fusion.69
  50.4 3.6 reshape.227
  56.3 3.6 reshape.225
  63.1 18.4 %while.26 = (s32[]{:T(128)}, bf16[3,512,4,64]{1,3,2,0:T(8,128)(2,1)}, f32[3,4,512]{2,1,0:T(4,128)S(1)}, bf16[3,512,4,64]{1,3,2,0:T(8,128)(2,1)}, s32[3,512]{1,0:...) while((s32[]{:T(128)}, ...), condition=%wide.region_3.4_spmd, body=%wide.region_0.3_spmd.sunk | while | flops 282196480 | bytes 14756965 | solution.py:136
  66.2 3.0 fusion.140
  84.5 3.7 fusion.86
  88.9 57.4 %reduce-scatter.5.cloned.1.call-done = f32[1536,256]{1,0:T(8,128)} async-done(((f32[1536,1024]{1,0:T(8,128)}), f32[1536,256]{1,0:T(8,128)}) %reduce-scatter.5.cloned.1.call-update) | async-done | bytes 1572880 | tf_op jit(solution)/shard_map/reduce_scatter | solution.py:138
  149.3 10.4 %all-reduce.5 = (f32[1536]{0:T(1024)S(1)}, f32[1536]{0:T(1024)S(1)}) all-reduce(f32[1536]{0:T(1024)S(1)} %get-tuple-element.191, f32[1536]{0:T(1024)S(1)} %get-tuple-element.190), channel_id=1, replica_groups=mesh['dp'=8,'tensor'=4] {'tensor'}, use_global_device_ids=true, to_apply=%region_8.9 | all-reduce | flops 3072 | bytes 24576 | tf_op jit(solution)/shard_map/psum | solution.py:145
  162.5 29.6 %all-gather.7.cloned.1.call-done = bf16[1536,1024]{1,0:T(8,128)(2,1)} async-done(((bf16[1536,256]{1,0:T(8,128)(2,1)}), bf16[1536,1024]{1,0:T(8,128)(2,1)}) %all-gather.7.cloned.1.call-update) | async-done | bytes 3145744 | tf_op jit(solution)/shard_map/all_gather | solution.py:148
  192.1 19.5 %multiply_convert_fusion.1 = (bf16[1536,1024]{1,0:T(8,128)(2,1)S(1)}, f32[1536,1024]{1,0:T(8,128)}, f32[1536,1024]{1,0:T(8,128)}) fusion(f32[1024]{0:T(1024)S(1)} %convert_element_type.124, bf16[1536,1024]{1,0:T(8,128)(2,1)} %all-gather.7.cloned.1.call-done, bf16[1024,1024]{1,0:T(8,128)(2,1)S(1)} %copy-done), kind=kOutput, calls=%fused_computation.76 | convolution fusion | flops 3325034496 | bytes 20975616 | tf_op jit(solution)/shard_map/dot_general | solution.py:149
  213.4 5.3 fusion.87
  219.4 57.4 %reduce-scatter.7.cloned.1.call-done = f32[1536,256]{1,0:T(8,128)} async-done(((f32[1536,1024]{1,0:T(8,128)}), f32[1536,256]{1,0:T(8,128)}) %reduce-scatter.7.cloned.1.call-update) | async-done | bytes 1572880 | tf_op jit(solution)/shard_map/reduce_scatter | solution.py:151
  276.7 3.5 fusion.78
  280.3 10.1 %all-reduce.4 = (f32[1536]{0:T(1024)S(1)}, f32[1536]{0:T(1024)S(1)}) all-reduce(f32[1536]{0:T(1024)S(1)} %get-tuple-element.189, f32[1536]{0:T(1024)S(1)} %get-tuple-element.188), channel_id=1, replica_groups=mesh['dp'=8,'tensor'=4] {'tensor'}, use_global_device_ids=true, to_apply=%region_13.14 | all-reduce | flops 3072 | bytes 24576 | tf_op jit(solution)/shard_map/psum | solution.py:158
  293.0 10.1 %all-reduce.3 = (f32[1536]{0:T(1024)S(1)}, f32[1536]{0:T(1024)S(1)}) all-reduce(f32[1536]{0:T(1024)S(1)} %get-tuple-element.185, f32[1536]{0:T(1024)S(1)} %get-tuple-element.192), channel_id=1, replica_groups=mesh['dp'=8,'tensor'=4] {'tensor'}, use_global_device_ids=true, to_apply=%region_17.18 | all-reduce | flops 3072 | bytes 24576 | tf_op jit(solution)/shard_map/psum | solution.py:167
  303.2 3.1 fusion.80
  308.7 29.4 %all-gather.9.cloned.1.call-done = bf16[1536,1024]{1,0:T(8,128)(2,1)} async-done(((bf16[1536,256]{1,0:T(8,128)(2,1)}), bf16[1536,1024]{1,0:T(8,128)(2,1)}) %all-gather.9.cloned.1.call-update) | async-done | bytes 3145744 | tf_op jit(solution)/shard_map/all_gather | solution.py:172
  338.1 11.8 %convert_reduce_fusion = (f32[1024]{0:T(1024)S(1)}, bf16[1536,1024]{1,0:T(8,128)(2,1)S(1)}) fusion(f32[1536,1024]{1,0:T(8,128)} %get-tuple-element.260, f32[1536,1024]{1,0:T(8,128)} %get-tuple-element.277, f32[1024]{0:T(1024)S(1)} %convert_element_type.124, bf16[1536,1024]{1,0:T(8,128)(2,1)} %all-gather.9.cloned.1.call-done, bf16[1024,1024]{1,0:T(8,128)(2,1)} %param.35), kind=kOutput, calls=%fused_computation.74 | convolution fusion | flops 3247963136 | bytes 20979712 | tf_op jit(solution)/shard_map/dot_general | solution.py:19
  351.6 5.6 fusion.88
  357.2 58.0 %reduce-scatter.9.cloned.1.call-done = f32[1536,256]{1,0:T(8,128)} async-done(((f32[1536,1024]{1,0:T(8,128)}), f32[1536,256]{1,0:T(8,128)}) %reduce-scatter.9.cloned.1.call-update) | async-done | bytes 1572880 | tf_op jit(solution)/shard_map/reduce_scatter | solution.py:179
  415.2 3.4 multiply_reduce_fusion.1
  418.6 10.1 %all-reduce.2 = (f32[1536]{0:T(1024)S(1)}, f32[1536]{0:T(1024)S(1)}) all-reduce(f32[1536]{0:T(1024)S(1)} %get-tuple-element.183, f32[1536]{0:T(1024)S(1)} %get-tuple-element.186), channel_id=1, replica_groups=mesh['dp'=8,'tensor'=4] {'tensor'}, use_global_device_ids=true, to_apply=%region_22.23 | all-reduce | flops 3072 | bytes 24576 | tf_op jit(solution)/shard_map/psum | solution.py:186
  433.7 29.2 %all-gather.11.cloned.1.call-done = bf16[1536,1024]{1,0:T(8,128)(2,1)} async-done(((bf16[1536,256]{1,0:T(8,128)(2,1)}), bf16[1536,1024]{1,0:T(8,128)(2,1)}) %all-gather.11.cloned.1.call-update) | async-done | bytes 3145744 | tf_op jit(solution)/shard_map/all_gather | solution.py:191
  467.4 3.4 copy.60
  472.7 26.4 %while.27 = (s32[]{:T(128)}, bf16[3,512,4,64]{1,3,2,0:T(8,128)(2,1)}, bf16[3,512,4,64]{1,3,2,0:T(8,128)(2,1)}, bf16[3,512,4,64]{1,3,2,0:T(8,128)(2,1)S(1)}, bf16...) while((s32[]{:T(128)}, ...), condition=%wide.region_25.26_spmd, body=%wide.region_23.25_spmd.sunk | while | flops 688519680 | bytes 38344856 | solution.py:194
  504.9 5.5 convolution_convert_fusion
  510.6 8.6 fusion.91
  519.3 5.0 fusion.90
  534.9 37.7 %all-reduce = (f32[256]{0:T(256)}, f32[256]{0:T(256)}, f32[256]{0:T(256)}, f32[256]{0:T(256)}, f32[256]{0:T(256)}, /*index=5*/f32[1024]{0:T(1024)}, f32[256]{0:T(256)}, f32[256]{0:T(256)}, f32[256]{0:T(256)}) all-reduce(f32[256]{0:T(256)S(1)} %reduce_sum.184, f32[256]{0:T(256)S(1)} %reduce_sum.186, ...), channel_id=1, replica_groups=mesh['dp'=8,'tensor'=4] {'dp'}, use_global_device_ids=true, to_apply=%region_31.32 | all-reduce | flops 3072 | bytes 24576 | tf_op jit(solution)/shard_map/psum | solution.py:88
  574.9 375.0 %all-reduce.8.cloned.1.call-done = (f32[1024,256]{0,1:T(8,128)}, f32[1024,256]{0,1:T(8,128)}, f32[1024,256]{0,1:T(8,128)}, f32[256,1024]{1,0:T(8,128)}, f32[1024,1024]{1,0:T(8,128)}, /*index=5*/f32[1024,1024]{1,0:T(8,128)}) async-done(((f32[1024,256]{0,1:T(8,128)}, f32[1024,256]{0,1:T(8,128)}, f32[1024,256]{0,1:T(8,128)}, f32[256,1024]{1,0:T(8,128)}, f32[1024,1024]{1,0:T(8,128)}, ...) | async-done | bytes 12582928 | tf_op jit(solution)/shard_map/psum | solution.py:88
  957.4 4.9 copy.117
  (201 shorter events, 116.6 us)
Async XLA Ops:
  7.2 184.9 %copy-start = (bf16[1024,1024]{1,0:T(8,128)(2,1)S(1)}, bf16[1024,1024]{1,0:T(8,128)(2,1)}, u32[]{:S(2)}) copy-start(bf16[1024,1024]{1,0:T(8,128)(2,1)} %param.33) | copy-start | bytes 6291460
  7.2 6.6 copy-start.17
  7.2 34.0 %all-gather.5.cloned.1.call-start = ((), (), s32[]{:S(2)}) async-start(), calls=%async_computation.4 | async-start | bytes 3932160 | tf_op jit(solution)/shard_map/all_gather | solution.py:124
  8.0 138.3 %reduce-scatter.5.cloned.1.call-start = ((), (), s32[]{:S(2)}) async-start(), calls=%async_computation.5 | async-start | bytes 7864320 | tf_op jit(solution)/shard_map/reduce_scatter | solution.py:138
  81.5 3.0 copy-start.16
  88.2 103.9 %all-gather.7.cloned.1.call-start = ((), (), s32[]{:S(2)}) async-start(), calls=%async_computation.6 | async-start | bytes 3932160 | tf_op jit(solution)/shard_map/all_gather | solution.py:148
  88.9 73.6 %copy-start.20 = (bf16[1024]{0:T(1024)(128)(2,1)S(1)}, bf16[1024]{0:T(1024)(128)(2,1)}, u32[]{:S(2)}) copy-start(bf16[1024]{0:T(1024)(128)(2,1)} %param.34) | copy-start | bytes 6148
  162.4 114.3 %reduce-scatter.7.cloned.1.call-start = ((), (), s32[]{:S(2)}) async-start(), calls=%async_computation.7 | async-start | bytes 7864320 | tf_op jit(solution)/shard_map/reduce_scatter | solution.py:151
  192.1 21.3 %copy-start.24 = (bf16[1024,1024]{1,0:T(8,128)(2,1)S(1)}, bf16[1024,1024]{1,0:T(8,128)(2,1)}, u32[]{:S(2)}) copy-start(bf16[1024,1024]{1,0:T(8,128)(2,1)} %param.35) | copy-start | bytes 6291460
  211.6 1.8 copy-start.31
  218.7 119.4 %all-gather.9.cloned.1.call-start = ((), (), s32[]{:S(2)}) async-start(), calls=%async_computation.8 | async-start | bytes 3932160 | tf_op jit(solution)/shard_map/all_gather | solution.py:172
  308.4 106.8 %reduce-scatter.9.cloned.1.call-start = ((), (), s32[]{:S(2)}) async-start(), calls=%async_computation.9 | async-start | bytes 7864320 | tf_op jit(solution)/shard_map/reduce_scatter | solution.py:179
  349.9 1.7 copy-start.32
  357.1 58.0 %copy-start.2 = (f32[1536,256]{1,0:T(8,128)S(1)}, f32[1536,256]{1,0:T(8,128)}, u32[]{:S(2)}) copy-start(f32[1536,256]{1,0:T(8,128)} %get-tuple-element.261) | copy-start | bytes 4718596
  357.2 105.7 %all-gather.11.cloned.1.call-start = ((), (), s32[]{:S(2)}) async-start(), calls=%async_computation.10 | async-start | bytes 3932160 | tf_op jit(solution)/shard_map/all_gather | solution.py:191
  431.0 1.2 copy-start.4
  433.2 139.4 %reduce-scatter.11.cloned.1.call-start = ((), (), s32[]{:S(2)}) async-start(), calls=%async_computation.11 | async-start | bytes 3932160 | tf_op jit(solution)/shard_map/reduce_scatter | solution.py:208
  465.8 6.9 copy-start.3
  499.1 3.2 copy-start.7
  503.4 1.4 copy-start.18
  510.4 439.5 %all-reduce.8.cloned.1.call-start = ((), (), s32[]{:S(2)}) async-start(), calls=%async_computation.12 | async-start | bytes 25165824 | tf_op jit(solution)/shard_map/psum | solution.py:88
  510.6 8.7 copy-start.22
  510.6 8.7 copy-start.33
  519.3 5.0 copy-start.19
  519.3 5.0 copy-start.21
  526.9 1.8 copy-start.11
  526.9 3.3 copy-start.23
  532.2 40.4 %copy-start.5 = (f32[1536,256]{1,0:T(8,128)S(1)}, f32[1536,256]{1,0:T(8,128)}, u32[]{:S(2)}) copy-start(f32[1536,256]{1,0:T(8,128)} %copy-done.4) | copy-start | bytes 4718596
  949.9 5.2 copy-start.15
  949.9 6.5 copy-start.14
  957.4 4.9 copy-start.12
  957.4 7.0 copy-start.1
  (13 other events, 11.7 us)
Sparse Core Ops, SparseCore 0:
  9.6 31.6 all-gather.4
  88.4 57.8 reduce-scatter.4
  162.5 29.5 all-gather.6
  218.8 57.8 reduce-scatter.6
  308.5 29.4 all-gather.8
  357.3 57.8 reduce-scatter.8
  433.4 29.4 all-gather.10
  510.5 37.7 reduce-scatter.10
  554.8 395.0 all-reduce.7
where the time goes:
time: 981 us; the launch traced here: 971 us
  waiting for transfers between devices  663 us (68%)
  matrix products  114 us (12%)
  blocking collectives  78.5 us (8%)
  local copies, waits for them, and re-layouts  63.9 us (7%)
  other arithmetic  35.8 us (4%)
  between operations  14.4 us (1%)
    psum x1, waiting for transfers between devices, summed(): return lax.psum(parts, 'dp')  375 us
    reduce_scatter x1, waiting for transfers between devices, local(): lax.psum_scatter(against(dpre, w_in), 'tensor', scatter_dimension=1, tile...  58 us
    reduce_scatter x1, waiting for transfers between devices, local(): lax.psum_scatter(jnp.dot(hidden, w_down, preferred_element_type=jnp.float...  57.4 us
    reduce_scatter x1, waiting for transfers between devices, local(): lax.psum_scatter(jnp.dot(context, w_out, preferred_element_type=jnp.float...  57.4 us
    psum x1, blocking collectives, summed(): return lax.psum(parts, 'dp')  37.7 us
    unnamed x80, local copies, waits for them, and re-layouts  31.2 us
    all_gather x1, waiting for transfers between devices, local(): lax.all_gather(h_one.astype(jnp.bfloat16), 'tensor', axis=1, tiled=True)  29.6 us
    all_gather x1, waiting for transfers between devices, local(): lax.all_gather(dz_two.astype(jnp.bfloat16), 'tensor', axis=1, tiled=True)  29.4 us
  transfers between devices with their start and end apart: 9, of which 8 were waited for; matrix products, arithmetic and copies ran while one was open for 3% of the time, Pallas kernels for 0%

commit v1 on v0

--- a/solution.py
+++ b/solution.py
@@ -7,6 +7,12 @@
 LEN = 512
 epsilon = 1e-05
 masked_fill = -1000000000.0
+
+
+def in_order(parts, dim):
+    lengths = list(parts.shape[1:])
+    lengths[dim] *= parts.shape[0]
+    return jnp.moveaxis(parts, 0, dim).reshape(lengths)
 
 
 def over_rows(left, right):
@@ -145,7 +151,20 @@
     sums_one = lax.psum((jnp.sum(z_one, axis=1), jnp.sum(z_one * z_one, axis=1)), "tensor")
     n_one, inv_one = norm_from(z_one, sums_one, model_width)
     h_one = n_one * gain_one.astype(jnp.float32) + bias_one.astype(jnp.float32)
-    h_low = lax.all_gather(h_one.astype(jnp.bfloat16), "tensor", axis=1, tiled=True)
+    shard = h_one.astype(jnp.bfloat16)
+    count = lax.axis_size("tensor")
+    pairs = [(i, (i + 1) % count) for i in range(count)]
+    back = [(b, a) for a, b in pairs]
+    lower, upper = ([], [])
+    for step in range(count - 1):
+        if step % 2 == 0:
+            lower.append(lax.ppermute(lower[-1] if lower else shard, "tensor", pairs))
+        else:
+            upper.append(lax.ppermute(upper[-1] if upper else shard, "tensor", back))
+    blocks = jnp.stack([*lower[::-1], shard, *upper])
+    shift = lax.axis_index("tensor") - len(lower)
+    blocks = blocks[(jnp.arange(count) - shift) % count]
+    h_low = in_order(blocks, 1)
     pre_act = jnp.dot(h_low, w_in, preferred_element_type=jnp.float32) + b_in.astype(jnp.float32)
     hidden = jax.nn.gelu(pre_act, approximate=False).astype(jnp.bfloat16)
     feed_mine = lax.psum_scatter(

time: 981 us -> 995 us (1.014)
    all_gather x1 -> x0, waiting for transfers between devices: 29.6 us -> none  [local(): lax.all_gather(h_one.astype(jnp.bfloat16), 'tensor', axis=1, tiled=True)]
    ppermute x0 -> x3, waiting for transfers between devices: none -> 26.7 us  [the longest x2 26.7 us: local(): lower.append(lax.ppermute(lower[-1] if lower else shard, 'tensor', pairs))]
  transfers between devices with their start and end apart: 9 -> 11, of which waited for: 8 -> 9; matrix products, arithmetic and copies ran while one was open for 3% -> 3% of each run, Pallas kernels for 0% -> 0%
where the time goes in v1:
time: 995 us; the launch traced here: 985 us
  waiting for transfers between devices  661 us (66%)
  matrix products  114 us (11%)
  blocking collectives  78.5 us (8%)
  local copies, waits for them, and re-layouts  72.9 us (7%)
  other arithmetic  40.8 us (4%)
  between operations  14.7 us (1%)
    psum x1, waiting for transfers between devices, summed(): return lax.psum(parts, 'dp')  375 us
    reduce_scatter x1, waiting for transfers between devices, local(): lax.psum_scatter(jnp.dot(hidden, w_down, preferred_element_type=jnp.float...  58.2 us
    reduce_scatter x1, waiting for transfers between devices, local(): lax.psum_scatter(against(dpre, w_in), 'tensor', scatter_dimension=1, tile...  58 us
    reduce_scatter x1, waiting for transfers between devices, local(): lax.psum_scatter(jnp.dot(context, w_out, preferred_element_type=jnp.float...  57.4 us
    psum x1, blocking collectives, summed(): return lax.psum(parts, 'dp')  37.7 us
    unnamed x80, local copies, waits for them, and re-layouts  31.3 us
    all_gather x1, waiting for transfers between devices, local(): lax.all_gather(dz_two.astype(jnp.bfloat16), 'tensor', axis=1, tiled=True)  29.4 us
    all_gather x1, waiting for transfers between devices, local(): lax.all_gather(dz_one.astype(jnp.bfloat16), 'tensor', axis=1, tiled=True)  29.2 us
  transfers between devices with their start and end apart: 11, of which 9 were waited for; matrix products, arithmetic and copies ran while one was open for 3% of the time, Pallas kernels for 0%

profile of v1, /device:TPU:0, one launch (start us, length us, event | category | flops | bytes accessed | tf_op | source)
XLA Modules:
  0.0 984.9 jit_solution(14496282035718630677)
XLA Ops:
  14.8 26.5 %all-gather.4.cloned.1.call-done = bf16[1536,1024]{1,0:T(8,128)(2,1)} async-done(((bf16[1536,256]{1,0:T(8,128)(2,1)}), bf16[1536,1024]{1,0:T(8,128)(2,1)}) %all-gather.4.cloned.1.call-update) | async-done | bytes 3145744 | tf_op jit(solution)/shard_map/all_gather | solution.py:130
  41.2 5.2 fusion.69
  50.4 3.6 reshape.279
  56.3 3.6 reshape.277
  63.1 18.4 %while.26 = (s32[]{:T(128)}, bf16[3,512,4,64]{1,3,2,0:T(8,128)(2,1)}, f32[3,4,512]{2,1,0:T(4,128)S(1)}, bf16[3,512,4,64]{1,3,2,0:T(8,128)(2,1)}, s32[3,512]{1,0:...) while((s32[]{:T(128)}, ...), condition=%wide.region_3.4_spmd, body=%wide.region_0.3_spmd.sunk | while | flops 282196480 | bytes 14756965 | solution.py:142
  84.5 3.7 fusion.88
  88.9 57.4 %reduce-scatter.5.cloned.1.call-done = f32[1536,256]{1,0:T(8,128)} async-done(((f32[1536,1024]{1,0:T(8,128)}), f32[1536,256]{1,0:T(8,128)}) %reduce-scatter.5.cloned.1.call-update) | async-done | bytes 1572880 | tf_op jit(solution)/shard_map/reduce_scatter | solution.py:144
  149.3 10.4 %all-reduce.5 = (f32[1536]{0:T(1024)S(1)}, f32[1536]{0:T(1024)S(1)}) all-reduce(f32[1536]{0:T(1024)S(1)} %get-tuple-element.191, f32[1536]{0:T(1024)S(1)} %get-tuple-element.190), channel_id=1, replica_groups=mesh['dp'=8,'tensor'=4] {'tensor'}, use_global_device_ids=true, to_apply=%region_8.9 | all-reduce | flops 3072 | bytes 24576 | tf_op jit(solution)/shard_map/psum | solution.py:151
  164.2 16.9 %collective-permute-done = bf16[1536,256]{1,0:T(8,128)(2,1)} collective-permute-done((bf16[1536,256]{1,0:T(8,128)(2,1)}, bf16[1536,256]{1,0:T(8,128)(2,1)}, u32[]{:S(2)}, u32[]{:S(2)}) %collective-permute-start) | collective-permute-done | bytes 786464 | tf_op jit(solution)/shard_map/ppermute | solution.py:161
  183.0 9.8 collective-permute-done.1
  195.9 4.3 gather_fusion
  200.2 4.7 copy.57
  204.9 19.7 %multiply_convert_fusion.1 = (bf16[1536,1024]{1,0:T(8,128)(2,1)S(1)}, f32[1536,1024]{1,0:T(8,128)}, f32[1536,1024]{1,0:T(8,128)}) fusion(f32[1024]{0:T(1024)S(1)} %convert_element_type.124, bf16[1536,1024]{0,1:T(8,128)(2,1)} %bitcast.180, bf16[1024,1024]{1,0:T(8,128)(2,1)S(1)} %copy-done), kind=kOutput, calls=%fused_computation.77 | convolution fusion | flops 3325034496 | bytes 20975616 | tf_op jit(solution)/shard_map/dot_general | solution.py:168
  226.3 5.3 fusion.89
  232.3 58.2 %reduce-scatter.7.cloned.1.call-done = f32[1536,256]{1,0:T(8,128)} async-done(((f32[1536,1024]{1,0:T(8,128)}), f32[1536,256]{1,0:T(8,128)}) %reduce-scatter.7.cloned.1.call-update) | async-done | bytes 1572880 | tf_op jit(solution)/shard_map/reduce_scatter | solution.py:170
  290.4 3.5 fusion.80
  294.0 10.1 %all-reduce.4 = (f32[1536]{0:T(1024)S(1)}, f32[1536]{0:T(1024)S(1)}) all-reduce(f32[1536]{0:T(1024)S(1)} %get-tuple-element.189, f32[1536]{0:T(1024)S(1)} %get-tuple-element.188), channel_id=1, replica_groups=mesh['dp'=8,'tensor'=4] {'tensor'}, use_global_device_ids=true, to_apply=%region_13.14 | all-reduce | flops 3072 | bytes 24576 | tf_op jit(solution)/shard_map/psum | solution.py:177
  306.7 10.1 %all-reduce.3 = (f32[1536]{0:T(1024)S(1)}, f32[1536]{0:T(1024)S(1)}) all-reduce(f32[1536]{0:T(1024)S(1)} %get-tuple-element.185, f32[1536]{0:T(1024)S(1)} %get-tuple-element.192), channel_id=1, replica_groups=mesh['dp'=8,'tensor'=4] {'tensor'}, use_global_device_ids=true, to_apply=%region_17.18 | all-reduce | flops 3072 | bytes 24576 | tf_op jit(solution)/shard_map/psum | solution.py:186
  322.4 29.4 %all-gather.6.cloned.1.call-done = bf16[1536,1024]{1,0:T(8,128)(2,1)} async-done(((bf16[1536,256]{1,0:T(8,128)(2,1)}), bf16[1536,1024]{1,0:T(8,128)(2,1)}) %all-gather.6.cloned.1.call-update) | async-done | bytes 3145744 | tf_op jit(solution)/shard_map/all_gather | solution.py:191
  351.7 11.8 %convert_reduce_fusion = (f32[1024]{0:T(1024)S(1)}, bf16[1536,1024]{1,0:T(8,128)(2,1)S(1)}) fusion(f32[1536,1024]{1,0:T(8,128)} %get-tuple-element.260, f32[1536,1024]{1,0:T(8,128)} %get-tuple-element.277, f32[1024]{0:T(1024)S(1)} %convert_element_type.124, bf16[1536,1024]{1,0:T(8,128)(2,1)} %all-gather.6.cloned.1.call-done, bf16[1024,1024]{1,0:T(8,128)(2,1)} %param.35), kind=kOutput, calls=%fused_computation.75 | convolution fusion | flops 3247963136 | bytes 20979712 | tf_op jit(solution)/shard_map/dot_general | solution.py:25
  365.2 5.6 fusion.90
  370.9 58.0 %reduce-scatter.9.cloned.1.call-done = f32[1536,256]{1,0:T(8,128)} async-done(((f32[1536,1024]{1,0:T(8,128)}), f32[1536,256]{1,0:T(8,128)}) %reduce-scatter.9.cloned.1.call-update) | async-done | bytes 1572880 | tf_op jit(solution)/shard_map/reduce_scatter | solution.py:198
  428.9 3.4 multiply_reduce_fusion.1
  432.3 10.1 %all-reduce.2 = (f32[1536]{0:T(1024)S(1)}, f32[1536]{0:T(1024)S(1)}) all-reduce(f32[1536]{0:T(1024)S(1)} %get-tuple-element.183, f32[1536]{0:T(1024)S(1)} %get-tuple-element.186), channel_id=1, replica_groups=mesh['dp'=8,'tensor'=4] {'tensor'}, use_global_device_ids=true, to_apply=%region_22.23 | all-reduce | flops 3072 | bytes 24576 | tf_op jit(solution)/shard_map/psum | solution.py:205
  447.3 29.2 %all-gather.8.cloned.1.call-done = bf16[1536,1024]{1,0:T(8,128)(2,1)} async-done(((bf16[1536,256]{1,0:T(8,128)(2,1)}), bf16[1536,1024]{1,0:T(8,128)(2,1)}) %all-gather.8.cloned.1.call-update) | async-done | bytes 3145744 | tf_op jit(solution)/shard_map/all_gather | solution.py:210
  486.4 26.4 %while.27 = (s32[]{:T(128)}, bf16[3,512,4,64]{1,3,2,0:T(8,128)(2,1)}, bf16[3,512,4,64]{1,3,2,0:T(8,128)(2,1)}, bf16[3,512,4,64]{1,3,2,0:T(8,128)(2,1)S(1)}, bf16...) while((s32[]{:T(128)}, ...), condition=%wide.region_25.26_spmd, body=%wide.region_23.25_spmd.sunk | while | flops 688519680 | bytes 38344856 | solution.py:213
  518.5 5.4 convolution_convert_fusion
  524.2 8.6 fusion.92
  532.8 5.0 fusion.93
  548.5 37.7 %all-reduce = (f32[256]{0:T(256)}, f32[256]{0:T(256)}, f32[256]{0:T(256)}, f32[256]{0:T(256)}, f32[256]{0:T(256)}, /*index=5*/f32[1024]{0:T(1024)}, f32[256]{0:T(256)}, f32[256]{0:T(256)}, f32[256]{0:T(256)}) all-reduce(f32[256]{0:T(256)S(1)} %reduce_sum.184, f32[256]{0:T(256)S(1)} %reduce_sum.186, ...), channel_id=1, replica_groups=mesh['dp'=8,'tensor'=4] {'dp'}, use_global_device_ids=true, to_apply=%region_31.32 | all-reduce | flops 3072 | bytes 24576 | tf_op jit(solution)/shard_map/psum | solution.py:94
  588.4 375.1 %all-reduce.8.cloned.1.call-done = (f32[1024,256]{0,1:T(8,128)}, f32[1024,256]{0,1:T(8,128)}, f32[1024,256]{0,1:T(8,128)}, f32[256,1024]{1,0:T(8,128)}, f32[1024,1024]{1,0:T(8,128)}, /*index=5*/f32[1024,1024]{1,0:T(8,128)}) async-done(((f32[1024,256]{0,1:T(8,128)}, f32[1024,256]{0,1:T(8,128)}, f32[1024,256]{0,1:T(8,128)}, f32[256,1024]{1,0:T(8,128)}, f32[1024,1024]{1,0:T(8,128)}, ...) | async-done | bytes 12582928 | tf_op jit(solution)/shard_map/psum | solution.py:94
  970.9 4.9 copy.118
  (210 shorter events, 132.9 us)
Async XLA Ops:
  7.2 197.7 %copy-start = (bf16[1024,1024]{1,0:T(8,128)(2,1)S(1)}, bf16[1024,1024]{1,0:T(8,128)(2,1)}, u32[]{:S(2)}) copy-start(bf16[1024,1024]{1,0:T(8,128)(2,1)} %param.33) | copy-start | bytes 6291460
  7.2 6.7 copy-start.17
  7.2 34.0 %all-gather.4.cloned.1.call-start = ((), (), s32[]{:S(2)}) async-start(), calls=%async_computation.4 | async-start | bytes 3932160 | tf_op jit(solution)/shard_map/all_gather | solution.py:130
  8.0 138.3 %reduce-scatter.5.cloned.1.call-start = ((), (), s32[]{:S(2)}) async-start(), calls=%async_computation.5 | async-start | bytes 7864320 | tf_op jit(solution)/shard_map/reduce_scatter | solution.py:144
  81.5 3.0 copy-start.16
  88.3 202.2 %reduce-scatter.7.cloned.1.call-start = ((), (), s32[]{:S(2)}) async-start(), calls=%async_computation.6 | async-start | bytes 7864320 | tf_op jit(solution)/shard_map/reduce_scatter | solution.py:170
  88.9 92.2 %copy-start.20 = (bf16[1024]{0:T(1024)(128)(2,1)S(1)}, bf16[1024]{0:T(1024)(128)(2,1)}, u32[]{:S(2)}) copy-start(bf16[1024]{0:T(1024)(128)(2,1)} %param.34) | copy-start | bytes 6148
  162.4 18.7 %collective-permute-start = (bf16[1536,256]{1,0:T(8,128)(2,1)}, bf16[1536,256]{1,0:T(8,128)(2,1)}, u32[]{:S(2)}, u32[]{:S(2)}) collective-permute-start(bf16[1536,256]{1,0:T(8,128)(2,1)} %fusion.77), channel_id=1, source_target_pairs={{0,1},{1,2},{2,3},{3,0},{4,5},{5,6},{6,7},{7,4},{8,9},{9,10},{10,1... | collective-permute-start | bytes 2359304 | tf_op jit(solution)/shard_map/ppermute | solution.py:161
  162.4 20.6 %collective-permute-start.2 = (bf16[1536,256]{1,0:T(8,128)(2,1)}, bf16[1536,256]{1,0:T(8,128)(2,1)}, u32[]{:S(2)}, u32[]{:S(2)}) collective-permute-start(bf16[1536,256]{1,0:T(8,128)(2,1)} %fusion.77), channel_id=1, source_target_pairs={{1,0},{2,1},{3,2},{0,3},{5,4},{6,5},{7,6},{4,7},{9,8},{10,9},{11,1... | collective-permute-start | bytes 2359304 | tf_op jit(solution)/shard_map/ppermute | solution.py:163
  181.1 11.7 %collective-permute-start.1 = (bf16[1536,256]{1,0:T(8,128)(2,1)}, bf16[1536,256]{1,0:T(8,128)(2,1)}, u32[]{:S(2)}, u32[]{:S(2)}) collective-permute-start(bf16[1536,256]{1,0:T(8,128)(2,1)} %collective-permute-done), channel_id=1, source_target_pairs={{0,1},{1,2},{2,3},{3,0},{4,5},{5,6},{6,7},{7,4},{8,9},{9,10},{10,1... | collective-permute-start | bytes 2359304 | tf_op jit(solution)/shard_map/ppermute | solution.py:161
  204.9 21.4 %copy-start.24 = (bf16[1024,1024]{1,0:T(8,128)(2,1)S(1)}, bf16[1024,1024]{1,0:T(8,128)(2,1)}, u32[]{:S(2)}) copy-start(bf16[1024,1024]{1,0:T(8,128)(2,1)} %param.35) | copy-start | bytes 6291460
  224.5 1.8 copy-start.31
  231.6 120.1 %all-gather.6.cloned.1.call-start = ((), (), s32[]{:S(2)}) async-start(), calls=%async_computation.7 | async-start | bytes 3932160 | tf_op jit(solution)/shard_map/all_gather | solution.py:191
  322.1 106.8 %reduce-scatter.9.cloned.1.call-start = ((), (), s32[]{:S(2)}) async-start(), calls=%async_computation.8 | async-start | bytes 7864320 | tf_op jit(solution)/shard_map/reduce_scatter | solution.py:198
  363.6 1.7 copy-start.33
  370.8 58.1 %copy-start.2 = (f32[1536,256]{1,0:T(8,128)S(1)}, f32[1536,256]{1,0:T(8,128)}, u32[]{:S(2)}) copy-start(f32[1536,256]{1,0:T(8,128)} %get-tuple-element.261) | copy-start | bytes 4718596
  370.8 105.7 %all-gather.8.cloned.1.call-start = ((), (), s32[]{:S(2)}) async-start(), calls=%async_computation.9 | async-start | bytes 3932160 | tf_op jit(solution)/shard_map/all_gather | solution.py:210
  446.9 139.3 %reduce-scatter.11.cloned.1.call-start = ((), (), s32[]{:S(2)}) async-start(), calls=%async_computation.10 | async-start | bytes 3932160 | tf_op jit(solution)/shard_map/reduce_scatter | solution.py:227
  479.4 6.9 copy-start.3
  512.7 3.2 copy-start.7
  523.9 439.5 %all-reduce.8.cloned.1.call-start = ((), (), s32[]{:S(2)}) async-start(), calls=%async_computation.11 | async-start | bytes 25165824 | tf_op jit(solution)/shard_map/psum | solution.py:94
  524.2 8.6 copy-start.22
  524.2 8.6 copy-start.32
  532.8 5.0 copy-start.19
  532.8 5.0 copy-start.21
  540.4 1.8 copy-start.11
  540.4 3.3 copy-start.23
  545.7 40.4 %copy-start.5 = (f32[1536,256]{1,0:T(8,128)S(1)}, f32[1536,256]{1,0:T(8,128)}, u32[]{:S(2)}) copy-start(f32[1536,256]{1,0:T(8,128)} %copy-done.4) | copy-start | bytes 4718596
  963.4 5.2 copy-start.15
  963.4 6.5 copy-start.14
  970.9 4.9 copy-start.12
  970.9 7.0 copy-start.1
  (15 other events, 14.3 us)
Sparse Core Ops, SparseCore 0:
  9.6 31.6 all-gather.3
  88.4 57.8 reduce-scatter.4
  231.7 58.6 reduce-scatter.6
  322.2 29.4 all-gather.5
  371.0 57.8 reduce-scatter.8
  447.0 29.4 all-gather.7
  524.1 37.7 reduce-scatter.10
  568.4 395.0 all-reduce.7
